TPU v7x, 32 devices: a 4x4x1 block of a 4x4x8 slice. The times are simulated.
32 devices in a mesh: dp: 1 (over z), y: 4 (over y), x: 8 (over x, core).
Axes of the slice: x: 4, y: 4, z: 1, core: 2. Of those that a mesh axis runs over, the one named last changes fastest.
The devices are a block of a 4x4x8 slice.
Arguments:
- hidden: bfloat16 [256, 4096], P('dp', ('x', 'y'))
- ln1_gain: bfloat16 [4096], P(('x', 'y'))
- ln1_bias: bfloat16 [4096], P(('x', 'y'))
- w_qkv: bfloat16 [4096, 3, 32, 128], P('x', None, 'y')
- b_qkv: bfloat16 [3, 32, 128], P(None, ('y', 'x'))
- w_out: bfloat16 [32, 128, 4096], P('y', None, 'x')
- b_out: bfloat16 [4096], P(('x', 'y'))
- ln2_gain: bfloat16 [4096], P(('x', 'y'))
- ln2_bias: bfloat16 [4096], P(('x', 'y'))
- w_up: bfloat16 [4096, 16384], P('x', 'y')
- b_up: bfloat16 [16384], P(('y', 'x'))
- w_down: bfloat16 [16384, 4096], P('y', 'x')
- b_down: bfloat16 [4096], P(('x', 'y'))
- k_cache: bfloat16 [256, 256, 32, 128], P('dp', None, ('y', 'x'))
- v_cache: bfloat16 [256, 256, 32, 128], P('dp', None, ('y', 'x'))
- q_pos: int32 [256], P('dp')
- k_pos: int32 [256, 256], P('dp')
- k_valid: int32 [256, 256], P('dp')
Outputs:
- output 1: bfloat16 [256, 4096], P('dp', ('x', 'y'))
- output 2: bfloat16 [256, 32, 128], P('dp', ('y', 'x'))
- output 3: bfloat16 [256, 32, 128], P('dp', ('y', 'x'))
All inputs are finite; a program needn't handle non-finite values.
Results may differ from a plain program's by a relative error of at most 0.0129273.
Values are sent between devices in bfloat16 or wider.
A program may use at most 768 MiB of HBM per device.

v0:
```python
import math
import jax
import jax.numpy as jnp
from jax import lax
from jax.sharding import PartitionSpec as P

EPS = 1e-5


def alibi_slopes(num_heads):
    closest = 2 ** int(math.floor(math.log2(num_heads)))
    base_part = [2.0 ** (-8.0 * (index + 1) / closest) for index in range(closest)]
    extra_part = [2.0 ** (-4.0 * (2 * index + 1) / closest) for index in range(num_heads - closest)]
    return jnp.array(base_part + extra_part, dtype=jnp.float32)


def layer_norm_sharded(piece, gain, shift, hid_total):
    piece_f32 = piece.astype(jnp.float32)
    stats = jnp.stack([jnp.sum(piece_f32, axis=1), jnp.sum(piece_f32 * piece_f32, axis=1)], axis=1)
    stats = lax.psum(stats, ("x", "y"))
    mean = stats[:, 0:1] / hid_total
    variance = stats[:, 1:2] / hid_total - mean * mean
    return ((piece_f32 - mean) * lax.rsqrt(variance + EPS) * gain.astype(jnp.float32) + shift.astype(jnp.float32)).astype(jnp.bfloat16)


def local_attention(query, key_new, val_new, k_cache, v_cache, q_pos, k_pos, k_valid, head_slopes):
    score_scale = query.shape[-1] ** -0.5
    scores = jnp.einsum("bnd,btnd->bnt", query, k_cache, preferred_element_type=jnp.float32) * score_scale
    distance = (q_pos[:, None] - k_pos).astype(jnp.float32)
    scores = scores - head_slopes[None, :, None] * distance[:, None, :]
    scores = jnp.where(k_valid[:, None, :] > 0, scores, -1e30)
    self_score = jnp.einsum("bnd,bnd->bn", query, key_new, preferred_element_type=jnp.float32) * score_scale
    row_max = jnp.maximum(jnp.max(scores, axis=2), self_score)
    exp_scores = jnp.exp(scores - row_max[:, :, None])
    self_exp = jnp.exp(self_score - row_max)
    denominator = jnp.sum(exp_scores, axis=2) + self_exp
    weighted = jnp.einsum("bnt,btnd->bnd", exp_scores.astype(jnp.bfloat16), v_cache, preferred_element_type=jnp.float32)
    weighted = weighted + self_exp.astype(jnp.bfloat16).astype(jnp.float32)[:, :, None] * val_new.astype(jnp.float32)
    return (weighted / denominator[:, :, None]).astype(jnp.bfloat16)


def solution(mesh):
    x_size = mesh.shape["x"]
    y_size = mesh.shape["y"]
    hid_spec = P(("x", "y"))
    ff_spec = P(("y", "x"))
    cache_spec = P("dp", None, ("y", "x"), None)
    in_specs = (P("dp", ("x", "y")), hid_spec, hid_spec, P("x", None, "y", None), P(None, ("y", "x"), None), P("y", None, "x"), hid_spec, hid_spec, hid_spec, P("x", "y"), ff_spec, P("y", "x"), hid_spec, cache_spec, cache_spec, P("dp"), P("dp", None), P("dp", None))
    out_specs = (P("dp", ("x", "y")), P("dp", ("y", "x"), None), P("dp", ("y", "x"), None))

    def layer(hidden, ln1_gain, ln1_bias, w_qkv, b_qkv, w_out, b_out, ln2_gain, ln2_bias, w_up, b_up, w_down, b_down, k_cache, v_cache, q_pos, k_pos, k_valid):
        num_heads = k_cache.shape[2]
        hid_total = hidden.shape[1]
        local_heads = num_heads // (x_size * y_size)
        slopes = alibi_slopes(num_heads)

        def device_step(hidden, ln1_gain, ln1_bias, w_qkv, b_qkv, w_out, b_out, ln2_gain, ln2_bias, w_up, b_up, w_down, b_down, k_cache, v_cache, q_pos, k_pos, k_valid):
            x_index = lax.axis_index("x")
            y_index = lax.axis_index("y")
            head_slopes = lax.dynamic_slice_in_dim(slopes, (y_index * x_size + x_index) * local_heads, local_heads)
            normed = layer_norm_sharded(hidden, ln1_gain, ln1_bias, hid_total)
            normed_rows = lax.all_gather(normed, "y", axis=1, tiled=True)
            qkv_part = jnp.einsum("bk,kcnd->bcnd", normed_rows, w_qkv, preferred_element_type=jnp.float32).astype(jnp.bfloat16)
            qkv_sum = lax.psum_scatter(qkv_part, "x", scatter_dimension=2, tiled=True)
            qkv_heads = (qkv_sum.astype(jnp.float32) + b_qkv.astype(jnp.float32)[None]).astype(jnp.bfloat16)
            key_new = qkv_heads[:, 1]
            val_new = qkv_heads[:, 2]
            attended = local_attention(qkv_heads[:, 0], key_new, val_new, k_cache, v_cache, q_pos, k_pos, k_valid, head_slopes)
            heads_group = lax.all_gather(attended, "x", axis=1, tiled=True)
            out_part = jnp.einsum("bnd,ndk->bk", heads_group, w_out, preferred_element_type=jnp.float32).astype(jnp.bfloat16)
            attn_sum = lax.psum_scatter(out_part, "y", scatter_dimension=1, tiled=True)
            residual = (hidden.astype(jnp.float32) + attn_sum.astype(jnp.float32) + b_out.astype(jnp.float32)).astype(jnp.bfloat16)
            normed_mlp = layer_norm_sharded(residual, ln2_gain, ln2_bias, hid_total)
            mlp_rows = lax.all_gather(normed_mlp, "y", axis=1, tiled=True)
            up_part = jnp.dot(mlp_rows, w_up, preferred_element_type=jnp.float32).astype(jnp.bfloat16)
            up_sum = lax.psum_scatter(up_part, "x", scatter_dimension=1, tiled=True)
            activated = jax.nn.gelu(up_sum.astype(jnp.float32) + b_up.astype(jnp.float32), approximate=True).astype(jnp.bfloat16)
            act_group = lax.all_gather(activated, "x", axis=1, tiled=True)
            down_part = jnp.dot(act_group, w_down, preferred_element_type=jnp.float32).astype(jnp.bfloat16)
            down_sum = lax.psum_scatter(down_part, "y", scatter_dimension=1, tiled=True)
            result = (residual.astype(jnp.float32) + down_sum.astype(jnp.float32) + b_down.astype(jnp.float32)).astype(jnp.bfloat16)
            return result, key_new, val_new

        return jax.shard_map(device_step, mesh=mesh, in_specs=in_specs, out_specs=out_specs, check_vma=False)(hidden, ln1_gain, ln1_bias, w_qkv, b_qkv, w_out, b_out, ln2_gain, ln2_bias, w_up, b_up, w_down, b_down, k_cache, v_cache, q_pos, k_pos, k_valid)

    return layer
```

profile of v0, /device:TPU:98, one launch (start us, length us, event | category | flops | bytes accessed | tf_op | source)
XLA Modules:
  0.0 351.2 jit_solution(12510918729816036221)
XLA Ops:
  7.3 1.1 convert_reduce_fusion.1
  8.4 46.9 %psum.14 = f32[256,2]{0,1:T(2,128)S(1)} all-reduce(f32[256,2]{0,1:T(2,128)S(1)} %pad_maximum_fusion), channel_id=1, replica_groups=mesh['dp'=1,'y'=4,'x'=8] {'x','y'}, use_global_device_ids=true, to_apply=%region_2.0 | all-reduce | flops 512 | bytes 4096 | tf_op jit(solution)/shard_map/psum | solution.py:20
  56.7 1.0 fusion.28
  57.7 12.7 %all_gather.12 = bf16[256,512]{1,0:T(8,128)(2,1)S(1)} all-gather(bf16[256,128]{1,0:T(8,128)(2,1)S(1)} %fusion.28), channel_id=1, replica_groups=mesh['dp'=1,'y'=4,'x'=8] {'y'}, dimensions={1}, use_global_device_ids=true | all-gather | bytes 327680 | tf_op jit(solution)/shard_map/all_gather | solution.py:62
  70.4 2.1 fusion.6
  73.9 55.9 %all-reduce.3.cloned.1.call-done = bf16[256,3,8,128]{3,0,2,1:T(8,128)(2,1)} async-done(((bf16[256,3,8,128]{3,0,2,1:T(8,128)(2,1)}), bf16[256,3,8,128]{3,0,2,1:T(8,128)(2,1)}) %all-reduce.3.cloned.1.call-update) | async-done | bytes 1572880
  129.8 1.6 constant_dynamic-slice_fusion
  132.5 10.9 %fusion.2 = f32[256,1,256]{2,1,0:T(1,128)} fusion(bf16[256,128,1]{1,2,0:T(2,128)(2,1)S(1)} %copy.33, bf16[256,256,1,128]{3,1,2,0:T(8,128)(2,1)} %param.32), kind=kOutput, calls=%fused_computation.2 | convolution fusion | flops 16777216 | bytes 17104896 | tf_op jit(solution)/shard_map/bnd,btnd->bnt/dot_general | solution.py:28
  143.4 2.0 fusion.47
  145.6 8.1 %fusion = f32[256,1,128]{2,1,0:T(1,128)S(1)} fusion(bf16[256,256,1,128]{3,1,2,0:T(8,128)(2,1)} %param.33, bf16[256,256,1]{1,0,2:T(8,128)(2,1)S(1)} %get-tuple-element.14), kind=kOutput, calls=%fused_computation | convolution fusion | flops 16777216 | bytes 17039360 | tf_op jit(solution)/shard_map/bnt,btnd->bnd/dot_general | solution.py:37
  155.4 24.2 %all-gather = bf16[256,1024]{0,1:T(8,128)(2,1)S(1)} all-gather(bf16[256,128]{0,1:T(8,128)(2,1)S(1)} %fusion.41), channel_id=2, replica_groups=mesh['dp'=1,'y'=4,'x'=8] {'x'}, dimensions={1}, use_global_device_ids=true | all-gather | bytes 589824 | tf_op jit(solution)/shard_map/all_gather | solution.py:69
  179.6 1.7 fusion.9
  182.9 18.7 %reduce-scatter.13.cloned.1.call-done = bf16[128,256]{1,0:T(8,128)(2,1)} async-done(((bf16[512,256]{1,0:T(8,128)(2,1)}), bf16[128,256]{1,0:T(8,128)(2,1)}) %reduce-scatter.13.cloned.1.call-update) | async-done | bytes 65552
  201.6 0.9 copy.45
  202.7 42.7 %psum.15 = f32[256,2]{0,1:T(2,128)S(1)} all-reduce(f32[256,2]{0,1:T(2,128)S(1)} %pad_maximum_fusion.1), channel_id=1, replica_groups=mesh['dp'=1,'y'=4,'x'=8] {'x','y'}, use_global_device_ids=true, to_apply=%region_9.10 | all-reduce | flops 512 | bytes 4096 | tf_op jit(solution)/shard_map/psum | solution.py:20
  245.5 12.9 %all_gather.14 = bf16[256,512]{1,0:T(8,128)(2,1)S(1)} all-gather(bf16[256,128]{1,0:T(8,128)(2,1)S(1)} %fusion.35), channel_id=1, replica_groups=mesh['dp'=1,'y'=4,'x'=8] {'y'}, dimensions={1}, use_global_device_ids=true | all-gather | bytes 327680 | tf_op jit(solution)/shard_map/all_gather | solution.py:74
  258.4 4.8 %convolution_convert_fusion = bf16[256,4096]{1,0:T(8,128)(2,1)} fusion(bf16[256,512]{1,0:T(8,128)(2,1)S(1)} %all_gather.14, bf16[512,4096]{1,0:T(8,128)(2,1)} %param.28), kind=kOutput, calls=%fused_computation.4 | convolution fusion | flops 1074790400 | bytes 6553600 | tf_op jit(solution)/shard_map/dot_general | solution.py:75
  263.4 29.0 %reduce-scatter.11.cloned.1.call-done = bf16[256,512]{1,0:T(8,128)(2,1)} async-done(((bf16[256,4096]{1,0:T(8,128)(2,1)}), bf16[256,512]{1,0:T(8,128)(2,1)}) %reduce-scatter.11.cloned.1.call-update) | async-done | bytes 262160 | tf_op jit(solution)/shard_map/reduce_scatter | solution.py:76
  292.4 1.9 fusion.17
  294.4 23.6 %all-gather.3.cloned.1.call-done = bf16[256,4096]{1,0:T(8,128)(2,1)} async-done(((bf16[256,512]{1,0:T(8,128)(2,1)}), bf16[256,4096]{1,0:T(8,128)(2,1)}) %all-gather.3.cloned.1.call-update) | async-done | bytes 2097168 | tf_op jit(solution)/shard_map/all_gather | solution.py:78
  317.9 4.1 %convolution_convert_fusion.1 = bf16[256,512]{1,0:T(8,128)(2,1)S(1)} fusion(bf16[256,4096]{1,0:T(8,128)(2,1)} %all-gather.3.cloned.1.call-done, bf16[4096,512]{1,0:T(8,128)(2,1)} %param.30), kind=kOutput, calls=%fused_computation.9 | convolution fusion | flops 1073872896 | bytes 6553600 | tf_op jit(solution)/shard_map/dot_general | solution.py:79
  322.9 1.6 copy.30
  325.2 17.8 %reduce-scatter.15.cloned.1.call-done = bf16[128,256]{1,0:T(8,128)(2,1)} async-done(((bf16[512,256]{1,0:T(8,128)(2,1)}), bf16[128,256]{1,0:T(8,128)(2,1)}) %reduce-scatter.15.cloned.1.call-update) | async-done | bytes 65552
  343.0 0.9 copy.47
  (62 shorter events, 10.2 us)
Async XLA Ops:
  7.2 63.2 %copy-start = (bf16[512,3,8,128]{3,2,1,0:T(8,128)(2,1)S(1)}, bf16[512,3,8,128]{3,2,1,0:T(8,128)(2,1)}, u32[]{:S(2)}) copy-start(bf16[512,3,8,128]{3,2,1,0:T(8,128)(2,1)} %param.22) | copy-start | bytes 9437188
  7.2 65.5 %copy-start.10 = (f32[32]{0:T(128)S(1)}, f32[32]{0:T(128)}, u32[]{:S(2)}) copy-start(f32[32]{0:T(128)} %constant.42.clone) | copy-start | bytes 388
  7.2 66.1 %copy-start.9 = (u32[32]{0:T(128)S(1)}, u32[32]{0:T(128)}, u32[]{:S(2)}) copy-start(u32[32]{0:T(128)} %constant.49) | copy-start | bytes 388
  7.2 66.6 %copy-start.3 = (bf16[3,1,128]{2,0,1:T(4,128)(2,1)S(1)}, bf16[3,1,128]{2,0,1:T(4,128)(2,1)}, u32[]{:S(2)}) copy-start(bf16[3,1,128]{2,0,1:T(4,128)(2,1)} %param.23) | copy-start | bytes 2308
  7.2 122.6 %all-reduce.3.cloned.1.call-start = ((), (), s32[]{:S(2)}) async-start(), calls=%async_computation.7 | async-start | bytes 3145728
  72.6 129.0 %reduce-scatter.13.cloned.1.call-start = ((), (), s32[]{:S(2)}) async-start(), calls=%async_computation.5 | async-start | bytes 327680
  132.5 10.9 %copy-start.5 = (s32[256]{0:T(256)S(1)}, s32[256]{0:T(256)}, u32[]{:S(2)}) copy-start(s32[256]{0:T(256)} %param.34) | copy-start | bytes 3076
  145.6 36.6 %copy-start.6 = (bf16[128]{0:T(256)(128)(2,1)S(1)}, bf16[128]{0:T(256)(128)(2,1)}, u32[]{:S(2)}) copy-start(bf16[128]{0:T(256)(128)(2,1)} %param.25) | copy-start | bytes 772
  145.6 36.7 %copy-start.7 = (bf16[128]{0:T(256)(128)(2,1)S(1)}, bf16[128]{0:T(256)(128)(2,1)}, u32[]{:S(2)}) copy-start(bf16[128]{0:T(256)(128)(2,1)} %param.26) | copy-start | bytes 772
  145.6 56.9 %copy-start.1 = (bf16[256,128]{1,0:T(8,128)(2,1)S(1)}, bf16[256,128]{1,0:T(8,128)(2,1)}, u32[]{:S(2)}) copy-start(bf16[256,128]{1,0:T(8,128)(2,1)} %param.19) | copy-start | bytes 196612
  182.1 110.2 %reduce-scatter.11.cloned.1.call-start = ((), (), s32[]{:S(2)}) async-start(), calls=%async_computation.3 | async-start | bytes 2359296 | tf_op jit(solution)/shard_map/reduce_scatter | solution.py:76
  258.4 5.0 %copy-start.4 = (bf16[512]{0:T(512)(128)(2,1)S(1)}, bf16[512]{0:T(512)(128)(2,1)}, u32[]{:S(2)}) copy-start(bf16[512]{0:T(512)(128)(2,1)} %param.29) | copy-start | bytes 3076
  263.3 54.7 %all-gather.3.cloned.1.call-start = ((), (), s32[]{:S(2)}) async-start(), calls=%async_computation.4 | async-start | bytes 2359296 | tf_op jit(solution)/shard_map/all_gather | solution.py:78
  294.3 28.6 %copy-start.8 = (bf16[128]{0:T(256)(128)(2,1)S(1)}, bf16[128]{0:T(256)(128)(2,1)}, u32[]{:S(2)}) copy-start(bf16[128]{0:T(256)(128)(2,1)} %param.31) | copy-start | bytes 772
  294.3 30.2 %copy-start.2 = (bf16[256,1,128]{0,2,1:T(8,128)(2,1)S(1)}, bf16[256,1,128]{0,2,1:T(8,128)(2,1)}, u32[]{:S(2)}) copy-start(bf16[256,1,128]{0,2,1:T(8,128)(2,1)} %get-tuple-element.15) | copy-start | bytes 196612
  294.3 48.7 %reduce-scatter.15.cloned.1.call-start = ((), (), s32[]{:S(2)}) async-start(), calls=%async_computation.6 | async-start | bytes 327680
Sparse Core Ops, SparseCore 0:
  72.7 57.0 all-reduce.2
  182.3 19.2 reduce-scatter.12
  263.4 28.9 reduce-scatter.10
  294.4 23.4 all-gather.2
  323.0 19.9 reduce-scatter.14
where the time goes:
time: 352 us; the launch traced here: 351 us
  waiting for transfers between devices  145 us (41%)
  blocking collectives  139 us (39%)
  matrix products  31.7 us (9%)
  between operations  14.1 us (4%)
  local copies, waits for them, and re-layouts  10.4 us (3%)
  other arithmetic  10.2 us (3%)
    unnamed x8, waiting for transfers between devices  92.7 us
    psum x2, blocking collectives, layer_norm_sharded(): stats = lax.psum(stats, ('x', 'y'))  89.6 us
    reduce_scatter x1, waiting for transfers between devices, device_step(): up_sum = lax.psum_scatter(up_part, 'x', scatter_dimension=1, tiled=True)  29 us
    all_gather x1, blocking collectives, device_step(): heads_group = lax.all_gather(attended, 'x', axis=1, tiled=True)  24.2 us
    all_gather x1, waiting for transfers between devices, device_step(): act_group = lax.all_gather(activated, 'x', axis=1, tiled=True)  23.6 us
    all_gather x1, blocking collectives, device_step(): mlp_rows = lax.all_gather(normed_mlp, 'y', axis=1, tiled=True)  12.9 us
    all_gather x1, blocking collectives, device_step(): normed_rows = lax.all_gather(normed, 'y', axis=1, tiled=True)  12.7 us
    dot_general x1, matrix products, local_attention(): jnp.einsum('bnd,btnd->bnt', query, k_cache, preferred_element_type=jnp.fl...  10.9 us
  transfers between devices with their start and end apart: 5, of which 5 were waited for; matrix products, arithmetic and copies ran while one was open for 1% of the time, Pallas kernels for 0%

commit v1 on v0

v1 whole, which is shorter than its diff:
```python
import functools
import math
import jax
import jax.numpy as jnp
from jax import lax
from jax.experimental import pallas as pl
from jax.experimental.pallas import tpu as pltpu
from jax.sharding import PartitionSpec as P

EPS = 1e-5
CORES = 2
MESH = pl.DeviceIdType.MESH
F32 = jnp.float32
BF16 = jnp.bfloat16


def alibi_slopes(num_heads):
    closest = 2 ** int(math.floor(math.log2(num_heads)))
    base_part = [2.0 ** (-8.0 * (index + 1) / closest) for index in range(closest)]
    extra_part = [2.0 ** (-4.0 * (2 * index + 1) / closest) for index in range(num_heads - closest)]
    return base_part + extra_part


def dot(left, right):
    return jnp.dot(left, right, preferred_element_type=F32)


class Links:
    def __init__(self, send_sems, recv_sems):
        self.send_sems, self.recv_sems = send_sems, recv_sems
        self.used = 0
        self.started = []

    def send(self, src, dst, device):
        copy = pltpu.make_async_remote_copy(
            src_ref=src, dst_ref=dst, send_sem=self.send_sems.at[self.used], recv_sem=self.recv_sems.at[self.used],
            device_id=device, device_id_type=MESH)
        self.used += 1
        copy.start()
        self.started.append(copy)
        return copy

    def drain(self):
        for copy in self.started:
            copy.wait_send()
        self.started = []


class RingSum:
    def __init__(self, links, own, travel, landed, up, down, pos, count):
        self.links, self.own, self.travel, self.landed = links, own, travel, landed
        self.up, self.down, self.pos = up, down, pos
        self.ahead, self.behind, self.far = lax.rem(pos + 1, count), lax.rem(pos + count - 1, count), lax.rem(pos + 2, count)

    def push(self, slot, value, device):
        self.travel[slot] = value.astype(BF16)
        return self.links.send(self.travel.at[slot], self.landed.at[slot], device)

    def first_far(self):
        self.far_a = self.push(0, self.own(self.far, 0), self.up)
        self.far_b = self.push(1, self.own(self.far, 1), self.down)

    def first_near(self):
        self.near_b = self.push(2, self.own(self.ahead, 1), self.up)
        self.near_a = self.push(3, self.own(self.behind, 0), self.down)

    def relay(self):
        self.far_a.wait_recv()
        self.comb_a = self.push(4, self.own(self.ahead, 0) + self.landed[0].astype(F32), self.up)
        self.far_b.wait_recv()
        self.comb_b = self.push(5, self.own(self.behind, 1) + self.landed[1].astype(F32), self.down)

    def final(self):
        self.near_a.wait_recv()
        self.comb_a.wait_recv()
        half_a = self.own(self.pos, 0) + self.landed[3].astype(F32) + self.landed[4].astype(F32)
        self.near_b.wait_recv()
        self.comb_b.wait_recv()
        half_b = self.own(self.pos, 1) + self.landed[2].astype(F32) + self.landed[5].astype(F32)
        return half_a, half_b


class RingGather:
    def __init__(self, links, buf, slot, half, up, down, pos, count, sibling=None):
        self.links, self.buf, self.slot, self.half, self.up, self.down = links, buf, slot, half, up, down
        self.pos, self.sibling = pos, sibling
        self.ahead, self.behind, self.far = lax.rem(pos + 1, count), lax.rem(pos + count - 1, count), lax.rem(pos + 2, count)
        self.sib = []

    def view(self, pos, part):
        return self.buf.at[self.slot(pos), pl.ds(part * self.half, self.half)]

    def send(self, pos, part, device):
        view = self.view(pos, part)
        return self.links.send(view, view, device)

    def cross(self, pos, part):
        if self.sibling is not None:
            self.sib.append(self.send(pos, part, self.sibling))

    def first(self):
        self.up_a = self.send(self.pos, 0, self.up)
        self.down_b = self.send(self.pos, 1, self.down)
        self.up_b = self.send(self.pos, 1, self.up)
        self.down_a = self.send(self.pos, 0, self.down)
        self.cross(self.pos, 0)
        self.cross(self.pos, 1)

    def relay(self):
        self.up_a.wait_recv()
        self.far_a = self.send(self.behind, 0, self.up)
        self.cross(self.behind, 0)
        self.down_b.wait_recv()
        self.far_b = self.send(self.ahead, 1, self.down)
        self.cross(self.ahead, 1)

    def near(self):
        self.up_b.wait_recv()
        self.cross(self.behind, 1)
        self.down_a.wait_recv()
        self.cross(self.ahead, 0)

    def last(self):
        self.far_a.wait_recv()
        self.cross(self.far, 0)
        self.far_b.wait_recv()
        self.cross(self.far, 1)

    def wait_cross(self, first, count):
        for copy in self.sib[first:first + count]:
            copy.wait_recv()


def kernel(xs, ys, slopes, hid_total,
           hidden, vecs, w_qkv, w_out, w_up, w_down, k_cache, v_cache, q_pos, k_pos, k_valid,
           out, k_new, v_new,
           kmem, vmem, wraw, wtmp, wq, wo, wu, wd, qpos_v, kpos_v, valid_v,
           xg, hg, vecg, stat1, stat2, act,
           qkv_send, qkv_sib, qkv_travel, qkv_land, qbuf,
           score, dist, mask, prob, obuf, attg,
           ysend, ytravel, yland, up_send, up_sib, up_travel, up_land, upg, dacc, dtravel, dland,
           send_sems, recv_sems, load_sems):
    x_index, y_index = lax.axis_index("x"), lax.axis_index("y")
    chips = xs // CORES
    chip, core = x_index // CORES, lax.rem(x_index, CORES)
    other = 1 - core
    rows = hidden.shape[0]
    half = rows // 2
    wide = hidden.shape[1]
    ctx = k_cache.shape[1]
    hdim = k_cache.shape[2]
    group = 16
    links = Links(send_sems, recv_sems)

    def at(x, y):
        return {"x": x, "y": y}

    sibling = at(CORES * chip + other, y_index)
    x_up = at(CORES * lax.rem(chip + 1, chips) + core, y_index)
    x_down = at(CORES * lax.rem(chip + chips - 1, chips) + core, y_index)
    y_up = at(x_index, lax.rem(y_index + 1, ys))
    y_down = at(x_index, lax.rem(y_index + ys - 1, ys))
    peers = [at(lax.rem(x_index + dx, xs), lax.rem(y_index + dy, ys)) for dy in range(ys) for dx in range(xs)][1:]

    barrier = pltpu.get_barrier_semaphore()
    for peer in peers:
        pl.semaphore_signal(barrier, inc=1, device_id=peer, device_id_type=MESH)

    loads = []

    def load(src, dst):
        copy = pltpu.make_async_copy(src, dst, load_sems.at[len(loads)])
        loads.append(copy)
        copy.start()
        return copy

    ld_x = load(hidden, xg.at[y_index])
    ld_vec = load(vecs, vecg.at[y_index])
    ld_pos = [load(q_pos, qpos_v), load(k_pos, kpos_v), load(k_valid, valid_v)]
    ld_wq = load(w_qkv, wraw)
    pieces = 8
    step = rows // pieces
    ld_k = [load(k_cache.at[pl.ds(i * step, step)], kmem.at[pl.ds(i * step, step)]) for i in range(pieces)]
    ld_v = [load(v_cache.at[pl.ds(i * step, step)], vmem.at[pl.ds(i * step, step)]) for i in range(pieces)]
    ld_wo, ld_wu, ld_wd = load(w_out, wo), load(w_up, wu), load(w_down, wd)

    lane = lax.broadcasted_iota(jnp.int32, (rows, 128), 1)

    def own_stats(piece, stat):
        piece = piece.astype(F32)
        total = jnp.sum(piece, axis=1, keepdims=True)
        squares = jnp.sum(piece * piece, axis=1, keepdims=True)
        both = jnp.where(lane == 0, total, jnp.where(lane == 1, squares, 0.0))
        stat[y_index * xs + x_index] = both.T[0:2, :]

    def send_stats(stat):
        mine = stat.at[y_index * xs + x_index]
        return [links.send(mine, mine, peer) for peer in peers]

    def normalize(stat, arrivals, buf, gain_row):
        for copy in arrivals:
            copy.wait_recv()
        total = jnp.sum(stat[...], axis=0)
        mean = total[0:1, :] / hid_total
        variance = total[1:2, :] / hid_total - mean * mean
        scale = lax.rsqrt(variance + EPS)
        sub = lax.broadcasted_iota(jnp.int32, (128, rows), 0)
        both = jnp.where(sub == 0, mean, scale).T
        mean_col, scale_col = both[:, 0:1], both[:, 1:2]
        for piece in range(ys):
            gain = vecg[piece, gain_row:gain_row + 1, :]
            shift = vecg[piece, gain_row + 1:gain_row + 2, :]
            value = (buf[piece].astype(F32) - mean_col) * scale_col * gain + shift
            act[:, piece * wide:(piece + 1) * wide] = value.astype(BF16)

    ld_x.wait()
    own_stats(xg[y_index], stat1)
    ld_vec.wait()
    pl.semaphore_wait(barrier, len(peers))

    stats = send_stats(stat1)
    gather = RingGather(links, xg, lambda pos: pos, half, y_up, y_down, y_index, ys)
    gather.first()
    vec_copies = [links.send(vecg.at[y_index], vecg.at[y_index], at(x_index, lax.rem(y_index + dy, ys))) for dy in range(1, ys)]

    ld_wq.wait()
    kblock = wtmp.shape[1] // xs

    @pl.loop(0, w_qkv.shape[0] // kblock)
    def _(block):
        start = pl.multiple_of(block * kblock, kblock)
        for c in range(3):
            wtmp[c] = wraw[pl.ds(start, kblock), c].astype(F32).reshape(kblock * xs, hdim)
        for c in range(3):
            for n in range(xs):
                part = wtmp[c, pl.ds(n, kblock, stride=xs), :].astype(BF16)
                wq[c * chips + n // CORES, pl.ds(start, kblock), (n % CORES) * hdim:(n % CORES + 1) * hdim] = part

    gather.relay()

    for copy in ld_pos:
        copy.wait()
    head = y_index * xs + x_index
    slope = jnp.float32(0.0)
    for index, value in enumerate(slopes):
        slope = jnp.where(head == index, jnp.float32(value), slope)
    dist[...] = slope * (qpos_v[...] - kpos_v[...].T).astype(F32)
    mask[...] = valid_v[...].astype(F32).T

    gather.near()
    gather.last()
    for copy in vec_copies:
        copy.wait_recv()
    normalize(stat1, stats, xg, 0)

    order = [lax.rem(chip + 2, chips), lax.rem(chip + 1, chips), lax.rem(chip + chips - 1, chips), chip]

    def qkv_product(c):
        arrivals = []
        for j in order:
            part = dot(act[...], wq[c * chips + j]).astype(BF16)
            for p in range(CORES):
                qkv_send[c, CORES * j + p] = part[:, p * hdim:(p + 1) * hdim]
            arrivals.append(links.send(qkv_send.at[c, CORES * j + other], qkv_sib.at[c, j], sibling))
        return arrivals

    def qkv_own(c):
        def own(j, part):
            view = pl.ds(part * half, half)
            return qkv_send[c, CORES * j + core, view].astype(F32) + qkv_sib[c, j, view].astype(F32)
        return own

    def qkv_ring(c):
        return RingSum(links, qkv_own(c), qkv_travel.at[c], qkv_land.at[c], x_up, x_down, chip, chips)

    def qkv_finish(ring, c):
        bias = vecg[y_index, 6 + c:7 + c, :]
        for part, value in enumerate(ring.final()):
            value = value.astype(BF16).astype(F32) + bias
            qbuf[c, part * half:(part + 1) * half, :] = value.astype(BF16)

    q_arr = qkv_product(0)
    q_ring, k_ring, v_ring = qkv_ring(0), qkv_ring(1), qkv_ring(2)
    q_arr[0].wait_recv()
    q_ring.first_far()
    for copy in q_arr[1:]:
        copy.wait_recv()
    q_ring.first_near()
    k_arr = qkv_product(1)
    q_ring.relay()
    for copy in k_arr:
        copy.wait_recv()
    k_ring.first_far()
    k_ring.first_near()
    v_arr = qkv_product(2)
    qkv_finish(q_ring, 0)

    for copy in ld_k:
        copy.wait()
    score_scale = hdim ** -0.5
    lanes = lax.broadcasted_iota(jnp.int32, (hdim, 128), 1)

    def query_t(part):
        return qbuf[0, part * half:(part + 1) * half, :].astype(F32).T

    def scores(part):
        q_t = query_t(part)
        columns = slice(part * half, (part + 1) * half)
        score[:, columns] = jnp.zeros((ctx, half), F32)

        @pl.loop(0, half // group)
        def _(block):
            base = part * half + block * group
            keys = jnp.concatenate([kmem[base + i] for i in range(group)], axis=1)
            picks = jnp.concatenate([jnp.where(lanes == block * group + i, q_t, 0.0).astype(BF16) for i in range(group)], axis=0)
            score[:, columns] += dot(keys, picks)

    scores(0)
    k_ring.relay()
    for copy in v_arr:
        copy.wait_recv()
    v_ring.first_far()
    v_ring.first_near()
    scores(1)
    qkv_finish(k_ring, 1)
    v_ring.relay()

    extras = []
    for part in range(2):
        columns = slice(part * half, (part + 1) * half)
        k_t = qbuf[1, columns, :].astype(F32).T
        self_score = jnp.sum(query_t(part) * k_t, axis=0, keepdims=True) * score_scale
        value = score[:, columns] * score_scale - dist[:, columns]
        value = jnp.where(mask[:, columns] > 0.0, value, -1e30)
        row_max = jnp.maximum(jnp.max(value, axis=0, keepdims=True), self_score)
        value = jnp.exp(value - row_max)
        self_exp = jnp.exp(self_score - row_max)
        denominator = jnp.sum(value, axis=0, keepdims=True) + self_exp
        prob[columns, :] = value.astype(BF16).astype(F32).T
        sub = lax.broadcasted_iota(jnp.int32, (128, half), 0)
        both = jnp.where(sub == 0, self_exp.astype(BF16).astype(F32), denominator).T
        extras.append((both[:, 0:1], both[:, 1:2]))

    for copy in ld_v:
        copy.wait()
    row = lax.broadcasted_iota(jnp.int32, (group, ctx), 0)

    @pl.loop(0, rows // group)
    def _(block):
        base = pl.multiple_of(block * group, group)
        weights = prob[pl.ds(base, group), :]
        picks = jnp.concatenate([jnp.where(row == i, weights, 0.0).astype(BF16) for i in range(group)], axis=1)
        values = vmem[pl.ds(base, group)].reshape(group * ctx, hdim)
        obuf[pl.ds(base, group), :] = dot(picks, values)

    qkv_finish(v_ring, 2)
    for part in range(2):
        columns = slice(part * half, (part + 1) * half)
        self_exp, denominator = extras[part]
        value = obuf[columns, :] + self_exp * qbuf[2, columns, :].astype(F32)
        attg[x_index, columns, :] = (value / denominator).astype(BF16)
    k_new[...] = qbuf[1]
    v_new[...] = qbuf[2]

    gather = RingGather(links, attg, lambda pos: CORES * pos + core, half, x_up, x_down, chip, chips, sibling)
    gather.first()
    gather.relay()
    gather.near()
    gather.last()
    gather.wait_cross(0, 8)

    ld_wo.wait()
    attended = jnp.concatenate([attg[n] for n in range(xs)], axis=1)
    for j in range(0, ys, 2):
        weights = wo[:, :, j * wide:(j + 2) * wide].reshape(xs * hdim, 2 * wide)
        part = dot(attended, weights).astype(BF16)
        ysend[j] = part[:, :wide]
        ysend[j + 1] = part[:, wide:]

    def y_own(j, part):
        return ysend[j, pl.ds(part * half, half)].astype(F32)

    ring = RingSum(links, y_own, ytravel, yland, y_up, y_down, y_index, ys)
    ring.first_far()
    ring.first_near()
    ring.relay()
    for part, value in enumerate(ring.final()):
        view = slice(part * half, (part + 1) * half)
        value = xg[y_index, view].astype(F32) + value.astype(BF16).astype(F32) + vecg[y_index, 4:5, :]
        hg[y_index, view] = value.astype(BF16)

    own_stats(hg[y_index], stat2)
    stats = send_stats(stat2)
    gather = RingGather(links, hg, lambda pos: pos, half, y_up, y_down, y_index, ys)
    gather.first()
    gather.relay()
    ld_wu.wait()
    gather.near()
    gather.last()
    normalize(stat2, stats, hg, 2)

    ff = up_send.shape[2]
    tile = 256
    up_arr = []
    for j in order:
        for p in (other, core):
            n = CORES * j + p
            for t in range(0, ff, tile):
                part = dot(act[...], wu[:, pl.ds(pl.multiple_of(n * ff + t, tile), tile)])
                up_send[n, :, t:t + tile] = part.astype(BF16)
            if p is other:
                up_arr.append(links.send(up_send.at[n], up_sib.at[j], sibling))

    def up_own(j, part):
        view = pl.ds(part * half, half)
        return up_send[CORES * j + core, view].astype(F32) + up_sib[j, view].astype(F32)

    ring = RingSum(links, up_own, up_travel, up_land, x_up, x_down, chip, chips)
    up_arr[0].wait_recv()
    ring.first_far()
    for copy in up_arr[1:]:
        copy.wait_recv()
    ring.first_near()
    ring.relay()
    bias = jnp.concatenate([vecg[y_index, 9 + i:10 + i, :] for i in range(ff // 128)], axis=1)
    for part, value in enumerate(ring.final()):
        value = jax.nn.gelu(value.astype(BF16).astype(F32) + bias, approximate=True)
        upg[x_index, part * half:(part + 1) * half, :] = value.astype(BF16)

    gather = RingGather(links, upg, lambda pos: CORES * pos + core, half, x_up, x_down, chip, chips, sibling)
    gather.first()
    ld_wd.wait()

    def down(slot, first):
        for t in range(0, dacc.shape[1], tile):
            part = dot(upg[slot], wd[pl.ds(pl.multiple_of(slot * ff, ff), ff), t:t + tile])
            if first:
                dacc[:, t:t + tile] = part
            else:
                dacc[:, t:t + tile] += part

    ahead, behind, far = gather.ahead, gather.behind, gather.far
    down(x_index, True)
    gather.wait_cross(0, 2)
    down(CORES * chip + other, False)
    gather.relay()
    gather.near()
    down(CORES * behind + core, False)
    down(CORES * ahead + core, False)
    gather.wait_cross(2, 4)
    down(CORES * behind + other, False)
    down(CORES * ahead + other, False)
    gather.last()
    down(CORES * far + core, False)
    gather.wait_cross(6, 2)
    down(CORES * far + other, False)

    for j in range(ys):
        ysend[j] = dacc[:, j * wide:(j + 1) * wide].astype(BF16)
    ring = RingSum(links, y_own, dtravel, dland, y_up, y_down, y_index, ys)
    ring.first_far()
    ring.first_near()
    ring.relay()
    for part, value in enumerate(ring.final()):
        view = slice(part * half, (part + 1) * half)
        value = hg[y_index, view].astype(F32) + value.astype(BF16).astype(F32) + vecg[y_index, 5:6, :]
        out[view, :] = value.astype(BF16)
    links.drain()


def solution(mesh):
    xs = mesh.shape["x"]
    ys = mesh.shape["y"]
    chips = xs // CORES
    hid_spec = P(("x", "y"))
    ff_spec = P(("y", "x"))
    cache_spec = P("dp", None, ("y", "x"), None)
    in_specs = (P("dp", ("x", "y")), hid_spec, hid_spec, P("x", None, "y", None), P(None, ("y", "x"), None), P("y", None, "x"), hid_spec, hid_spec, hid_spec, P("x", "y"), ff_spec, P("y", "x"), hid_spec, cache_spec, cache_spec, P("dp"), P("dp", None), P("dp", None))
    out_specs = (P("dp", ("x", "y")), P("dp", ("y", "x"), None), P("dp", ("y", "x"), None))

    def layer(hidden, ln1_gain, ln1_bias, w_qkv, b_qkv, w_out, b_out, ln2_gain, ln2_bias, w_up, b_up, w_down, b_down, k_cache, v_cache, q_pos, k_pos, k_valid):
        num_heads = k_cache.shape[2]
        hid_total = hidden.shape[1]
        slopes = alibi_slopes(num_heads)

        def device_step(hidden, ln1_gain, ln1_bias, w_qkv, b_qkv, w_out, b_out, ln2_gain, ln2_bias, w_up, b_up, w_down, b_down, k_cache, v_cache, q_pos, k_pos, k_valid):
            rows, wide = hidden.shape
            ctx, hdim = k_cache.shape[1], k_cache.shape[3]
            ff = b_up.shape[0]
            half = rows // 2
            small = [ln1_gain, ln1_bias, ln2_gain, ln2_bias, b_out, b_down]
            vecs = jnp.concatenate([v.reshape(1, wide) for v in small] + [b_qkv.reshape(3, hdim), b_up.reshape(ff // wide, wide)], axis=0)
            vecs = jnp.pad(vecs.astype(F32), ((0, -vecs.shape[0] % 8), (0, 0)))
            k_cache = k_cache.reshape(rows, ctx, hdim)
            v_cache = v_cache.reshape(rows, ctx, hdim)
            vm = pltpu.VMEM
            kblock = 64
            scratch = [
                vm(k_cache.shape, BF16), vm(v_cache.shape, BF16), vm(w_qkv.shape, BF16), vm((3, kblock * xs, hdim), F32),
                vm((3 * chips, w_qkv.shape[0], CORES * hdim), BF16), vm(w_out.shape, BF16), vm(w_up.shape, BF16), vm(w_down.shape, BF16),
                vm((1, rows), jnp.int32), vm(k_pos.shape, jnp.int32), vm(k_valid.shape, jnp.int32),
                vm((ys, rows, wide), BF16), vm((ys, rows, wide), BF16), vm((ys,) + vecs.shape, F32),
                vm((xs * ys, 2, rows), F32), vm((xs * ys, 2, rows), F32), vm((rows, ys * wide), BF16),
                vm((3, xs, rows, hdim), BF16), vm((3, chips, rows, hdim), BF16), vm((3, 6, half, hdim), BF16), vm((3, 6, half, hdim), BF16), vm((3, rows, hdim), BF16),
                vm((ctx, rows), F32), vm((ctx, rows), F32), vm((ctx, rows), F32), vm((rows, ctx), F32), vm((rows, hdim), F32), vm((xs, rows, hdim), BF16),
                vm((ys, rows, wide), BF16), vm((6, half, wide), BF16), vm((6, half, wide), BF16),
                vm((xs, rows, ff), BF16), vm((chips, rows, ff), BF16), vm((6, half, ff), BF16), vm((6, half, ff), BF16), vm((xs, rows, ff), BF16),
                vm((rows, ys * wide), F32), vm((6, half, wide), BF16), vm((6, half, wide), BF16),
                pltpu.SemaphoreType.DMA((180,)), pltpu.SemaphoreType.DMA((180,)), pltpu.SemaphoreType.DMA((32,)),
            ]
            any_spec = pl.BlockSpec(memory_space=pl.ANY)
            vm_spec = pl.BlockSpec(memory_space=pltpu.VMEM)
            out, k_new, v_new = pl.pallas_call(
                functools.partial(kernel, xs, ys, slopes, hid_total),
                out_shape=[jax.ShapeDtypeStruct((rows, wide), BF16), jax.ShapeDtypeStruct((rows, hdim), BF16), jax.ShapeDtypeStruct((rows, hdim), BF16)],
                in_specs=[any_spec] * 11,
                out_specs=[vm_spec] * 3,
                scratch_shapes=scratch,
                compiler_params=pltpu.CompilerParams(collective_id=0, has_side_effects=True, vmem_limit_bytes=67043328),
            )(hidden, vecs, w_qkv, w_out, w_up, w_down, k_cache, v_cache, q_pos.reshape(1, rows), k_pos, k_valid)
            return out, k_new.reshape(rows, 1, hdim), v_new.reshape(rows, 1, hdim)

        return jax.shard_map(device_step, mesh=mesh, in_specs=in_specs, out_specs=out_specs, check_vma=False)(hidden, ln1_gain, ln1_bias, w_qkv, b_qkv, w_out, b_out, ln2_gain, ln2_bias, w_up, b_up, w_down, b_down, k_cache, v_cache, q_pos, k_pos, k_valid)

    return layer
```

time: 352 us -> 101 us (0.29)
  waiting for transfers between devices: 145 us -> 0 us
  blocking collectives: 139 us -> 0 us
  Pallas kernels: 0 us -> 92.5 us
  matrix products: 31.7 us -> 0 us
  between operations: 14.1 us -> 0.64 us
  other arithmetic: 10.2 us -> 0.6 us
  local copies, waits for them, and re-layouts: 10.4 us -> 6.66 us
    unnamed x8 -> x0, waiting for transfers between devices: 92.7 us -> none
    pallas_call x0 -> x1, Pallas kernels: none -> 92.5 us  [device_step(): pl.pallas_call(functools.partial(kernel, xs, ys, slopes, hid_total), out_...]
    psum x2 -> x0, blocking collectives: 89.6 us -> none  [layer_norm_sharded(): stats = lax.psum(stats, ('x', 'y'))]
    all_gather x3 -> x0, blocking collectives: 49.7 us -> none  [the longest x1 24.2 us: device_step(): heads_group = lax.all_gather(attended, 'x', axis=1, tiled=True)]
    dot_general x6 -> x0, matrix products: 31.7 us -> none  [the longest x1 10.9 us: local_attention(): jnp.einsum('bnd,btnd->bnt', query, k_cache, preferred_element_type=jnp.fl...]
    reduce_scatter x1 -> x0, waiting for transfers between devices: 29 us -> none  [device_step(): up_sum = lax.psum_scatter(up_part, 'x', scatter_dimension=1, tiled=True)]
    all_gather x1 -> x0, waiting for transfers between devices: 23.6 us -> none  [device_step(): act_group = lax.all_gather(activated, 'x', axis=1, tiled=True)]
    convert_element_type x14 -> x0, other arithmetic: 6.68 us -> none  [the longest x1 1.85 us: device_step(): jax.nn.gelu(up_sum.astype(jnp.float32) + b_up.astype(jnp.float32), approx...]
  transfers between devices with their start and end apart: 5 -> 0, of which waited for: 5 -> 0; matrix products, arithmetic and copies ran while one was open for 1% -> 0% of each run, Pallas kernels for 0% -> 0%
where the time goes in v1:
time: 101 us; the launch traced here: 100 us
  Pallas kernels  92.5 us (92%)
  local copies, waits for them, and re-layouts  6.66 us (7%)
    pallas_call x1, Pallas kernels, device_step(): pl.pallas_call(functools.partial(kernel, xs, ys, slopes, hid_total), out_...  92.5 us
    unnamed x3, local copies, waits for them, and re-layouts  4.42 us
    concatenate x1, local copies, waits for them, and re-layouts, device_step(): jnp.concatenate([v.reshape(1, wide) for v in small] + [b_qkv.reshape(3, h...  2.24 us

profile of v1, /device:TPU:98, one launch (start us, length us, event | category | flops | bytes accessed | tf_op | source)
XLA Modules:
  0.0 100.4 jit_solution(14181018053854434487)
XLA Ops:
  0.6 2.2 %concatenate.3 = bf16[13,128]{1,0:T(8,128)(2,1)S(1)} concatenate(bf16[1,128]{1,0:T(2,128)(2,1)} %bitcast.20, bf16[1,128]{1,0:T(2,128)(2,1)} %bitcast.21, bf16[1,128]{1,0:T(2,128)(2,1)} %bitcast.22, bf16[1,128]{1,0:T(2,128)(2,1)} %bitcast.23, bf16[1,128]{1,0:T(2,128)(2,1)} %bitcast.24, bf16[1,128]{1,0:T(2,128)(2,1)} %bitcast.25, bf16[3,128]{1,0:T(4,128)(2,1)} %bitcast.18, ...), dimensions={0} | concatenate | bytes 6656 | tf_op jit(solution)/shard_map/concatenate | solution.py:492
  2.9 0.6 pad_convert_fusion.vecs
  3.5 92.5 %shard_map.193 = (bf16[256,128]{1,0:T(8,128)(2,1)}, bf16[256,128]{1,0:T(8,128)(2,1)}, bf16[256,128]{1,0:T(8,128)(2,1)}) custom-call(bf16[256,128]{1,0:T(8,128)(2,1)} %hidden.1, f32[16,128]{1,0:T(8,128)} %pad_convert_fusion.vecs, bf16[512,3,8,128]{3,2,1,0:T(8,128)(2,1)} %w_qkv.1, bf16[8,128,512]{2,1,0:T(8,128)(2,1)} %w_out.1, bf16[512,4096]{1,0:T(8,128)(2,1)} %w_up.1, ...), custom_call_target="tpu_custom_call" | custom-call | tf_op jit(solution)/shard_map/pallas_call | solution.py:513
  95.9 1.5 %copy.24 = bf16[256,128]{1,0:T(8,128)(2,1)} copy(bf16[256,128]{1,0:T(8,128)(2,1)} %get-tuple-element.12) | data formatting | bytes 131072
  97.4 1.5 %copy.25 = bf16[256,1,128]{2,0,1:T(8,128)(2,1)} copy(bf16[256,1,128]{2,0,1:T(8,128)(2,1)} %bitcast.16) | data formatting | bytes 131072
  98.9 1.5 %copy.26 = bf16[256,1,128]{2,0,1:T(8,128)(2,1)} copy(bf16[256,1,128]{2,0,1:T(8,128)(2,1)} %bitcast.15) | data formatting | bytes 131072
